TPU v7x, 32 devices: a whole 2x2x4 slice. The times are simulated.
32 devices in a mesh: dp: 8 (over z, x), mp: 4 (over y, core).
Axes of the slice: x: 2, y: 2, z: 4, core: 2. Of those that a mesh axis runs over, the one named last changes fastest.
Arguments:
- text_in: bfloat16 [7680, 768], P(('dp', 'mp')), may hold values from -6 to 6
- caption_ids: int32 [480, 16], P('dp'), may hold values from 0 to 31999, as said below
- pairing: int32 [480], replicated, may hold values from 0 to 479, each once
- image_low: bfloat16 [19200, 768], P(('dp', 'mp')), may hold values from -6 to 6
- image_high: bfloat16 [13920, 768], P(('dp', 'mp')), may hold values from -6 to 6
- img_gains: float32 [2, 768], replicated, may hold values from 0.5 to 1.5
- img_qkv: bfloat16 [3, 768, 768], P(None, None, 'mp'), may hold values from -0.21875 to 0.21875
- img_out: bfloat16 [768, 768], P('mp'), may hold values from -0.625 to 0.625
- img_fc1: bfloat16 [768, 3072], P(None, 'mp'), may hold values from -0.21875 to 0.21875
- img_fc2: bfloat16 [3072, 768], P('mp'), may hold values from -0.109375 to 0.109375
- txt_qkv: bfloat16 [3, 768, 768], P(None, None, 'mp'), may hold values from -0.21875 to 0.21875
- txt_qv_bias: float32 [2, 768], P(None, 'mp'), may hold values from -3 to 3
- txt_out: bfloat16 [768, 768], P('mp'), may hold values from -0.4375 to 0.4375
- txt_fc1: bfloat16 [768, 3072], P(None, 'mp'), may hold values from -0.21875 to 0.21875
- txt_fc1_bias: float32 [3072], P('mp'), may hold values from -3 to 3
- txt_fc2: bfloat16 [3072, 768], P('mp'), may hold values from -0.109375 to 0.109375
- txt_gains: float32 [2, 768], replicated, may hold values from 0.5 to 1.5
- txt_shifts: float32 [2, 768], replicated, may hold values from -2 to 2
- txt_biases: float32 [2, 768], replicated, may hold values from -2 to 2
Outputs:
- loss: float32 [], replicated
- grad_text_in: float32 [7680, 768], P(('dp', 'mp'))
- grad_qkv: float32 [3, 768, 768], P(None, None, 'mp')
- grad_qv_bias: float32 [2, 768], P(None, 'mp')
- grad_out: float32 [768, 768], P('mp')
- grad_fc1: float32 [768, 3072], P(None, 'mp')
- grad_fc1_bias: float32 [3072], P('mp')
- grad_fc2: float32 [3072, 768], P('mp')
- grad_gains: float32 [2, 768], replicated
- grad_shifts: float32 [2, 768], replicated
- grad_biases: float32 [2, 768], replicated
Inputs may be any that keep to these rules, and one draw needn't show every extreme that they name: `caption_ids`: in each caption the nonzero ids come first and the zeros after; each caption has 4 to 16 nonzero ids. Image i is paired with caption pairing[i]; each caption is paired once.
All inputs are finite; a program needn't handle non-finite values.
Results may differ from a plain program's by a relative error of at most 0.017.
Values may be sent and summed in bfloat16 or wider, within the bound.
A program may use at most 192 MiB of HBM per device.

v0:
```python
import jax
import jax.numpy as jnp
from jax import lax
from jax.sharding import PartitionSpec as P

D = 768
HEAD = 64
L = 16
P_LOW = 50
P_HIGH = 145
EPS = 1e-06
SCALE = 40.0
LOSS_SCALE = 16.0
MASKED = -1e30


def layer_stats(values):
    center = values - jnp.mean(values, -1, keepdims=True)
    inverse = lax.rsqrt(jnp.mean(center * center, -1, keepdims=True) + EPS)
    return (center * inverse, inverse)


def norm_back(grad_out, unit, inverse, gain):
    scaled = grad_out * gain
    return inverse * (
        scaled
        - jnp.mean(scaled, -1, keepdims=True)
        - unit * jnp.mean(scaled * unit, -1, keepdims=True)
    )


def gelu_exact(values):
    return jax.nn.gelu(values, approximate=False)


def score_rows(queries, keys_all, keep):
    scores = (
        jnp.einsum("nqhe,nkhe->nhqk", queries, keys_all, preferred_element_type=jnp.float32) * 0.125
    )
    if keep is not None:
        scores = jnp.where(keep, scores, MASKED)
    return scores


def attention_shares(queries, keys_all, keep):
    scores = score_rows(queries, keys_all, keep)
    highest = jnp.max(scores, -1, keepdims=True)
    raised = jnp.exp(scores - highest)
    totals = jnp.sum(raised, -1, keepdims=True)
    return (raised / totals, highest + jnp.log(totals))


def image_tower(tokens, count, length, gains, weights):
    w_qkv, w_out, w_fc1, w_fc2 = weights
    head_count = D // HEAD
    inputs = tokens.astype(jnp.float32)
    unit, spare = layer_stats(inputs)
    normed = (unit * gains[0]).astype(jnp.bfloat16)
    projected = jnp.einsum("rd,jdw->jrw", normed, w_qkv, preferred_element_type=jnp.float32).astype(
        jnp.bfloat16
    )
    shaped = projected.reshape(3, count, length, head_count, HEAD)
    shares, spare_lse = attention_shares(shaped[0], shaped[1], None)
    context = jnp.einsum(
        "nhqk,nkhe->nqhe",
        shares.astype(jnp.bfloat16),
        shaped[2],
        preferred_element_type=jnp.float32,
    )
    context = context.astype(jnp.bfloat16).reshape(count * length, D)
    middle = inputs + jnp.dot(context, w_out, preferred_element_type=jnp.float32)
    unit2, spare2 = layer_stats(middle)
    normed2 = (unit2 * gains[1]).astype(jnp.bfloat16)
    active = gelu_exact(jnp.dot(normed2, w_fc1, preferred_element_type=jnp.float32)).astype(
        jnp.bfloat16
    )
    result = middle + jnp.dot(active, w_fc2, preferred_element_type=jnp.float32)
    pooled = jnp.mean(result.reshape(count, length, D), 1)
    return (pooled * lax.rsqrt(jnp.sum(pooled * pooled, -1, keepdims=True) + EPS)).astype(
        jnp.bfloat16
    )


def local(
    text_in,
    caption_ids,
    pairing,
    image_low,
    image_high,
    img_gains,
    img_qkv,
    img_out,
    img_fc1,
    img_fc2,
    txt_qkv,
    txt_qv_bias,
    txt_out,
    txt_fc1,
    txt_fc1_bias,
    txt_fc2,
    txt_gains,
    txt_shifts,
    txt_biases,
):
    weights = (
        lax.all_gather(img_qkv, "mp", axis=2, tiled=True),
        lax.all_gather(img_out, "mp", axis=0, tiled=True),
        lax.all_gather(img_fc1, "mp", axis=1, tiled=True),
        lax.all_gather(img_fc2, "mp", axis=0, tiled=True),
    )
    low_count = image_low.shape[0] // P_LOW
    high_count = image_high.shape[0] // P_HIGH
    images16 = jnp.concatenate(
        [
            image_tower(image_low, low_count, P_LOW, img_gains, weights),
            image_tower(image_high, high_count, P_HIGH, img_gains, weights),
        ],
        0,
    )
    width = txt_qkv.shape[2]
    head_count = width // HEAD
    own_rows = text_in.shape[0]
    own_caps = own_rows // L
    group_caps = caption_ids.shape[0]
    group_rows = group_caps * L
    own_ids = lax.dynamic_slice_in_dim(caption_ids, lax.axis_index("mp") * own_caps, own_caps, 0)
    keep = (caption_ids > 0)[:, None, None, :]
    inputs = text_in.astype(jnp.float32)
    unit1, inverse1 = layer_stats(inputs)
    normed1 = (unit1 * txt_gains[0] + txt_shifts[0]).astype(jnp.bfloat16)
    bias_rows = jnp.stack([txt_qv_bias[0], jnp.zeros_like(txt_qv_bias[0]), txt_qv_bias[1]])
    piece = lax.all_gather(normed1, "mp", axis=0, tiled=True)
    made = jnp.einsum("rd,jdw->rjw", piece, txt_qkv, preferred_element_type=jnp.float32) + bias_rows
    joined = jnp.concatenate(
        [piece, made.astype(jnp.bfloat16).reshape(piece.shape[0], 3 * width)], 1
    )
    normed1_all = joined[:, :D]
    triple = joined[:, D:].reshape(group_caps, L, 3, head_count, HEAD)
    queries = triple[:, :, 0]
    keys_all = triple[:, :, 1]
    values_all = triple[:, :, 2]
    shares, log_totals = attention_shares(queries, keys_all, keep)
    context = jnp.einsum(
        "nhqk,nkhe->nqhe",
        shares.astype(jnp.bfloat16),
        values_all,
        preferred_element_type=jnp.float32,
    )
    context = context.astype(jnp.bfloat16).reshape(group_rows, width)
    middle = inputs + (
        lax.psum_scatter(
            jnp.dot(context, txt_out, preferred_element_type=jnp.float32).astype(jnp.bfloat16),
            "mp",
            scatter_dimension=0,
            tiled=True,
        ).astype(jnp.float32)
        + txt_biases[0]
    )
    unit2, inverse2 = layer_stats(middle)
    normed2 = (unit2 * txt_gains[1] + txt_shifts[1]).astype(jnp.bfloat16)
    piece = lax.all_gather(normed2, "mp", axis=0, tiled=True)
    hidden_piece = jnp.dot(piece, txt_fc1, preferred_element_type=jnp.float32) + txt_fc1_bias
    spread = jnp.concatenate([piece.astype(jnp.float32), hidden_piece], 1)
    normed2_all = spread[:, :D].astype(jnp.bfloat16)
    hidden = spread[:, D:]
    active, gelu_pull = jax.vjp(gelu_exact, hidden)
    active16 = active.astype(jnp.bfloat16)
    result = middle + (
        lax.psum_scatter(
            jnp.dot(active16, txt_fc2, preferred_element_type=jnp.float32).astype(jnp.bfloat16),
            "mp",
            scatter_dimension=0,
            tiled=True,
        ).astype(jnp.float32)
        + txt_biases[1]
    )
    present = (own_ids > 0).astype(jnp.float32)
    counts = jnp.sum(present, 1, keepdims=True)
    pooled = jnp.sum(result.reshape(own_caps, L, D) * present[:, :, None], 1) / counts
    inverse_len = lax.rsqrt(jnp.sum(pooled * pooled, -1, keepdims=True) + EPS)
    captions_unit = pooled * inverse_len
    captions16 = captions_unit.astype(jnp.bfloat16)
    total_pairs = pairing.shape[0]
    first_pair = lax.axis_index(("dp", "mp")) * own_caps
    arrived = lax.all_gather(captions16, ("dp", "mp"), axis=0, tiled=True)
    logits = SCALE * jnp.einsum("id,jd->ij", images16, arrived, preferred_element_type=jnp.float32)
    targets = lax.dynamic_slice_in_dim(pairing, first_pair, own_caps, 0)
    matched = (targets[:, None] == jnp.arange(total_pairs)[None, :]).astype(jnp.float32)
    raised = jnp.exp(logits - SCALE)
    local_lse = SCALE + jnp.log(jnp.sum(raised, 1))
    partial_value = jnp.sum(raised, 0)
    own_term = 0.5 * jnp.sum(local_lse) - jnp.sum(matched * logits)
    summed, scalar = lax.psum((partial_value, own_term), ("dp", "mp"))
    other_lse = SCALE + jnp.log(summed)
    total = scalar + 0.5 * jnp.sum(other_lse)
    loss = total / total_pairs
    grads16 = (
        LOSS_SCALE
        * (
            0.5 * jnp.exp(logits - local_lse[:, None])
            + 0.5 * jnp.exp(logits - other_lse[None, :])
            - matched
        )
    ).astype(jnp.bfloat16)
    grad_caps = lax.psum_scatter(
        SCALE * jnp.einsum("ic,id->cd", grads16, images16, preferred_element_type=jnp.float32),
        ("dp", "mp"),
        scatter_dimension=0,
        tiled=True,
    )
    grad_pooled = inverse_len * (
        grad_caps - captions_unit * jnp.sum(captions_unit * grad_caps, -1, keepdims=True)
    )
    grad_result = (grad_pooled[:, None, :] * (present / counts)[:, :, None]).reshape(own_rows, D)
    grad_all = lax.all_gather(grad_result.astype(jnp.bfloat16), "mp", axis=0, tiled=True)
    grad_fc2 = jnp.einsum("gf,gd->fd", active16, grad_all, preferred_element_type=jnp.float32)
    grad_active = jnp.einsum("gd,fd->gf", grad_all, txt_fc2, preferred_element_type=jnp.float32)
    grad_hidden16 = gelu_pull(grad_active)[0].astype(jnp.bfloat16)
    grad_fc1 = jnp.einsum(
        "gd,gf->df", normed2_all, grad_hidden16, preferred_element_type=jnp.float32
    )
    grad_fc1_bias = jnp.sum(grad_hidden16.astype(jnp.float32), 0)
    grad_normed2 = lax.psum_scatter(
        jnp.einsum("gf,df->gd", grad_hidden16, txt_fc1, preferred_element_type=jnp.float32).astype(
            jnp.bfloat16
        ),
        "mp",
        scatter_dimension=0,
        tiled=True,
    ).astype(jnp.float32)
    grad_middle = grad_result + norm_back(grad_normed2, unit2, inverse2, txt_gains[1])
    grad_mid_all = lax.all_gather(grad_middle.astype(jnp.bfloat16), "mp", axis=0, tiled=True)
    grad_out = jnp.einsum("gw,gd->wd", context, grad_mid_all, preferred_element_type=jnp.float32)
    grad_context = jnp.einsum(
        "gd,wd->gw", grad_mid_all, txt_out, preferred_element_type=jnp.float32
    )
    grad_context = grad_context.astype(jnp.bfloat16).reshape(group_caps, L, head_count, HEAD)
    shares_again = jnp.exp(score_rows(queries, keys_all, keep) - log_totals)
    grad_shares = jnp.einsum(
        "nqhe,nkhe->nhqk", grad_context, values_all, preferred_element_type=jnp.float32
    )
    grad_values = jnp.einsum(
        "nhqk,nqhe->nkhe",
        shares_again.astype(jnp.bfloat16),
        grad_context,
        preferred_element_type=jnp.float32,
    ).astype(jnp.bfloat16)
    grad_scores = (
        shares_again * (grad_shares - jnp.sum(grad_shares * shares_again, -1, keepdims=True))
    ).astype(jnp.bfloat16)
    grad_queries = (
        jnp.einsum("nhqk,nkhe->nqhe", grad_scores, keys_all, preferred_element_type=jnp.float32)
        * 0.125
    ).astype(jnp.bfloat16)
    grad_keys = (
        jnp.einsum("nhqk,nqhe->nkhe", grad_scores, queries, preferred_element_type=jnp.float32)
        * 0.125
    ).astype(jnp.bfloat16)
    grad_triple = jnp.stack([grad_queries, grad_keys, grad_values], 0).reshape(3, group_rows, width)
    grad_qkv = jnp.einsum(
        "gd,jgw->jdw", normed1_all, grad_triple, preferred_element_type=jnp.float32
    )
    grad_qv_bias = jnp.stack(
        [
            jnp.sum(grad_triple[0].astype(jnp.float32), 0),
            jnp.sum(grad_triple[2].astype(jnp.float32), 0),
        ]
    )
    grad_normed1 = lax.psum_scatter(
        jnp.einsum("jgw,jdw->gd", grad_triple, txt_qkv, preferred_element_type=jnp.float32).astype(
            jnp.bfloat16
        ),
        "mp",
        scatter_dimension=0,
        tiled=True,
    ).astype(jnp.float32)
    grad_inputs = grad_middle + norm_back(grad_normed1, unit1, inverse1, txt_gains[0])
    summed_grads = lax.psum(
        (grad_qkv, grad_qv_bias, grad_out, grad_fc1, grad_fc1_bias, grad_fc2), "dp"
    )
    small_parts = jnp.stack(
        [
            jnp.sum(grad_normed1 * unit1, 0),
            jnp.sum(grad_normed2 * unit2, 0),
            jnp.sum(grad_normed1, 0),
            jnp.sum(grad_normed2, 0),
            jnp.sum(grad_middle, 0),
            jnp.sum(grad_result, 0),
        ]
    )
    shared = lax.psum(small_parts, ("dp", "mp"))
    return (
        loss,
        grad_inputs,
        summed_grads[0],
        summed_grads[1],
        summed_grads[2],
        summed_grads[3],
        summed_grads[4],
        summed_grads[5],
        shared[0:2],
        shared[2:4],
        shared[4:6],
    )


def solution(mesh):
    placed = (
        P(("dp", "mp"), None),
        P("dp", None),
        P(),
        P(("dp", "mp"), None),
        P(("dp", "mp"), None),
        P(),
        P(None, None, "mp"),
        P("mp", None),
        P(None, "mp"),
        P("mp", None),
        P(None, None, "mp"),
        P(None, "mp"),
        P("mp", None),
        P(None, "mp"),
        P("mp"),
        P("mp", None),
        P(),
        P(),
        P(),
    )
    return jax.shard_map(
        local,
        mesh=mesh,
        in_specs=placed,
        out_specs=(
            P(),
            P(("dp", "mp"), None),
            P(None, None, "mp"),
            P(None, "mp"),
            P("mp", None),
            P(None, "mp"),
            P("mp"),
            P("mp", None),
            P(),
            P(),
            P(),
        ),
        check_vma=False,
    )
```

profile of v0, /device:TPU:0, one launch (start us, length us, event | category | flops | bytes accessed | tf_op | source)
XLA Modules:
  0.0 829.3 jit_solution(6300139161258848959)
XLA Ops:
  11.1 2.0 fusion.104
  14.9 20.2 %all-gather.18.cloned.1.call-done = bf16[960,768]{1,0:T(8,128)(2,1)} async-done(((bf16[240,768]{1,0:T(8,128)(2,1)}), bf16[960,768]{1,0:T(8,128)(2,1)}) %all-gather.18.cloned.1.call-update) | async-done | bytes 1474576 | tf_op jit(solution)/shard_map/all_gather | solution.py:132
  35.1 2.7 fusion.231
  39.0 1.9 copy.127
  40.9 3.0 reshape_reshape.3
  43.9 3.2 fusion.221
  50.4 1.6 convolution_convert_fusion.2
  59.0 20.6 %reduce-scatter.7.cloned.1.call-done = bf16[240,768]{1,0:T(8,128)(2,1)} async-done(((bf16[960,768]{1,0:T(8,128)(2,1)}), bf16[240,768]{1,0:T(8,128)(2,1)}) %reduce-scatter.7.cloned.1.call-update) | async-done | bytes 368656 | tf_op jit(solution)/shard_map/reduce_scatter | solution.py:151
  82.1 1.9 add_convert_fusion.2
  84.2 27.8 %all-gather.10.cloned.1.call-done = bf16[3,768,768]{1,2,0:T(8,128)(2,1)} async-done(((bf16[3,768,192]{1,2,0:T(8,128)(2,1)}), bf16[3,768,768]{1,2,0:T(8,128)(2,1)}) %all-gather.10.cloned.1.call-update) | async-done | bytes 3538960 | tf_op jit(solution)/shard_map/all_gather | solution.py:106
  112.0 4.5 convert_bitcast_fusion
  116.5 1.4 fusion.222
  117.9 4.5 squeeze.30
  122.4 4.1 squeeze.31
  126.5 3.8 fusion.45
  130.3 3.2 fusion.229
  133.5 2.8 squeeze.29
  136.3 4.5 convert_bitcast_fusion.1
  140.9 1.9 copy.118
  142.7 4.2 reshape.220
  146.9 2.7 fusion.230
  150.9 1.9 convert_bitcast_fusion.2
  154.1 2.5 reshape.236
  156.6 3.3 reshape.237
  159.9 2.4 fusion.65
  162.3 3.8 fusion.227
  166.2 2.3 reshape.235
  168.5 4.1 fusion.69
  173.6 2.1 reshape.222
  175.8 2.5 fusion.228
  179.6 29.0 %all-gather.16.cloned.1.call-done = bf16[3072,768]{1,0:T(8,128)(2,1)} async-done(((bf16[768,768]{1,0:T(8,128)(2,1)}), bf16[3072,768]{1,0:T(8,128)(2,1)}) %all-gather.16.cloned.1.call-update) | async-done | bytes 4718608 | tf_op jit(solution)/shard_map/all_gather | solution.py:109
  208.6 25.3 %fusion.58 = f32[600,768]{1,0:T(8,128)S(1)} fusion(f32[600,768]{1,0:T(8,128)} %copy-done.23, bf16[3072,768]{1,0:T(8,128)(2,1)} %all-gather.16.cloned.1.call-done, bf16[768,3072]{1,0:T(8,128)(2,1)} %all-gather.14.cloned.1.call-done, f32[768]{0:T(1024)S(1)} %get-tuple-element.22, f32[600]{0:T(1024)S(1)} %add_rsqrt_fusion, f32[600]{0:T(1024)S(1)} %broadcast_multiply_fusion), kind=kOutput, calls=%fused_computation.102 | convolution fusion | flops 5784422400 | bytes 13131456 | tf_op jit(solution)/shard_map/dot_general | solution.py:77
  234.0 10.1 %multiply_convert_fusion = (bf16[960,768]{1,0:T(8,128)(2,1)S(1)}, f32[960,768]{1,0:T(8,128)}, f32[960,768]{1,0:T(8,128)}) fusion(f32[768]{0:T(1024)S(1)} %copy-done.64, bf16[960,768]{1,0:T(8,128)(2,1)} %all-gather.20.cloned.1.call-done, bf16[768,768]{1,0:T(8,128)(2,1)S(1)} %copy-done), kind=kOutput, calls=%fused_computation.54 | convolution fusion | flops 1181122560 | bytes 10030080 | tf_op jit(solution)/shard_map/dot_general | solution.py:162
  245.3 2.4 convolution_convert_fusion.1
  248.0 20.6 %fusion.62 = f32[435,768]{1,0:T(8,128)} fusion(f32[435,768]{1,0:T(8,128)} %copy-done.25, bf16[3072,768]{1,0:T(8,128)(2,1)} %all-gather.16.cloned.1.call-done, bf16[768,3072]{1,0:T(8,128)(2,1)} %all-gather.14.cloned.1.call-done, f32[768]{0:T(1024)S(1)} %get-tuple-element.22, f32[435]{0:T(512)S(1)} %add_rsqrt_fusion.2, f32[435]{0:T(512)S(1)} %broadcast_multiply_fusion.2), kind=kOutput, calls=%fused_computation.115 | convolution fusion | flops 4193706240 | bytes 12116376 | tf_op jit(solution)/shard_map/dot_general | solution.py:77
  268.5 1.5 reshape.221
  270.1 1.8 reduce_sum.383
  271.9 1.5 reshape.223
  277.0 42.7 %all-gather = bf16[32,15,768]{2,1,0:T(8,128)(2,1)S(1)} all-gather(bf16[1,15,768]{2,1,0:T(8,128)(2,1)S(1)} %fusion.139), channel_id=1, replica_groups=mesh['dp'=8,'mp'=4] {'dp','mp'}, dimensions={0}, use_global_device_ids=true | all-gather | bytes 760320 | tf_op jit(solution)/shard_map/all_gather | solution.py:185
  319.9 1.6 fusion.137
  321.5 36.8 %psum.64 = f32[480]{0:T(512)S(1)} all-reduce(f32[480]{0:T(512)S(1)} %get-tuple-element.19), channel_id=1, replica_groups=mesh['dp'=8,'mp'=4] {'dp','mp'}, use_global_device_ids=true, to_apply=%region_32.33 | all-reduce | flops 480 | bytes 3840 | tf_op jit(solution)/shard_map/psum | solution.py:193
  360.7 77.1 %fusion = f32[16,768]{1,0:T(8,128)S(1)} fusion(f32[480,768]{1,0:T(8,128)S(1)} %convolution_multiply_fusion), kind=kCustom, calls=%all-reduce-scatter | all-reduce-scatter fusion | flops 393217 | bytes 1523712
  445.0 18.3 %all-gather.22.cloned.1.call-done = bf16[960,768]{1,0:T(8,128)(2,1)} async-done(((bf16[240,768]{1,0:T(8,128)(2,1)}), bf16[960,768]{1,0:T(8,128)(2,1)}) %all-gather.22.cloned.1.call-update) | async-done | bytes 1474576 | tf_op jit(solution)/shard_map/all_gather | solution.py:215
  463.3 5.6 convert_reduce_fusion
  470.1 2.5 convolution_convert_fusion
  472.6 27.5 %reduce-scatter.11.cloned.1.call-done = bf16[240,768]{1,0:T(8,128)(2,1)} async-done(((bf16[960,768]{1,0:T(8,128)(2,1)}), bf16[240,768]{1,0:T(8,128)(2,1)}) %reduce-scatter.11.cloned.1.call-update) | async-done | bytes 368656 | tf_op jit(solution)/shard_map/reduce_scatter | solution.py:223
  500.1 1.5 fusion.114
  505.8 18.1 %all-gather.24.cloned.1.call-done = bf16[960,768]{1,0:T(8,128)(2,1)} async-done(((bf16[240,768]{1,0:T(8,128)(2,1)}), bf16[960,768]{1,0:T(8,128)(2,1)}) %all-gather.24.cloned.1.call-update) | async-done | bytes 1474576 | tf_op jit(solution)/shard_map/all_gather | solution.py:232
  523.9 2.8 convolution_convert_fusion.5
  529.0 2.3 multiply_reduce_fusion.3
  537.2 2.0 copy.143
  539.2 1.6 copy.140
  542.1 2.0 copy.144
  545.4 3.9 bitcast_convert_fusion
  549.6 4.8 fusion.234
  554.5 2.8 fusion.233
  558.7 2.3 convolution_bitcast_fusion
  563.4 13.5 %reduce-scatter.13.cloned.1.call-done = bf16[240,768]{1,0:T(8,128)(2,1)} async-done(((bf16[960,768]{1,0:T(8,128)(2,1)}), bf16[240,768]{1,0:T(8,128)(2,1)}) %reduce-scatter.13.cloned.1.call-update) | async-done | bytes 368656 | tf_op jit(solution)/shard_map/reduce_scatter | solution.py:269
  576.9 1.4 fusion.115
  578.4 23.1 %all-reduce.3 = (f32[2,192]{1,0:T(2,128)}, f32[768]{0:T(1024)}) all-reduce(f32[2,192]{1,0:T(2,128)S(1)} %pad_maximum_fusion.7, f32[768]{0:T(1024)S(1)} %get-tuple-element.38), channel_id=1, replica_groups=mesh['dp'=8,'mp'=4] {'dp'}, use_global_device_ids=true, to_apply=%region_46.47 | all-reduce | flops 1152 | bytes 9216 | tf_op jit(solution)/shard_map/psum | solution.py:278
  601.5 41.9 %all-reduce.2 = (f32[]{:T(128)}, f32[6,768]{1,0:T(8,128)S(1)}) all-reduce(f32[]{:T(128)S(6)} %sub.157, f32[6,768]{1,0:T(8,128)S(1)} %stack.59), channel_id=1, replica_groups=mesh['dp'=8,'mp'=4] {'dp','mp'}, use_global_device_ids=true, to_apply=%region_30.31 | all-reduce | flops 4609 | bytes 36872 | tf_op jit(solution)/shard_map/psum | solution.py:193
  644.7 2.2 fusion.107
  646.8 168.1 %all-reduce.7.cloned.1.call-done = (f32[3,768,192]{1,2,0:T(8,128)}, f32[192,768]{1,0:T(8,128)}, f32[768,768]{1,0:T(8,128)}, f32[768,768]{1,0:T(8,128)}) async-done(((f32[3,768,192]{1,2,0:T(8,128)}, f32[192,768]{1,0:T(8,128)}, f32[768,768]{1,0:T(8,128)}, f32[768,768]{1,0:T(8,128)}), (f32[3,768,192]{1,2,0:T(8,128)}, f32[192,768]{1,0:T(8,128)}, f32[768,768]{1,0:T(8,128)}, ...) | async-done | bytes 7077904 | tf_op jit(solution)/shard_map/psum | solution.py:278
  814.9 2.9 copy.205
  (270 shorter events, 61.4 us)
Async XLA Ops:
  7.2 226.8 %copy-start = (bf16[768,768]{1,0:T(8,128)(2,1)S(1)}, bf16[768,768]{1,0:T(8,128)(2,1)}, u32[]{:S(2)}) copy-start(bf16[768,768]{1,0:T(8,128)(2,1)} %param.32) | copy-start | bytes 3538948
  7.2 27.9 %all-gather.18.cloned.1.call-start = ((), (), s32[]{:S(2)}) async-start(), calls=%async_computation.8 | async-start | bytes 1843200 | tf_op jit(solution)/shard_map/all_gather | solution.py:132
  8.5 2.1 copy-start.47
  10.5 71.6 %copy-start.43 = (f32[768]{0:T(1024)}, f32[768]{0:T(1024)S(1)}, u32[]{:S(2)}) copy-start(f32[768]{0:T(1024)S(1)} %get-tuple-element.82) | copy-start | bytes 9220
  13.1 66.5 %reduce-scatter.7.cloned.1.call-start = ((), (), s32[]{:S(2)}) async-start(), calls=%async_computation.9 | async-start | bytes 1843200 | tf_op jit(solution)/shard_map/reduce_scatter | solution.py:151
  52.1 2.6 copy-start.46
  52.1 5.1 copy-start.57
  52.1 5.2 copy-start.58
  52.1 5.8 copy-start.16
  52.1 6.0 copy-start.11
  52.1 59.9 %all-gather.10.cloned.1.call-start = ((), (), s32[]{:S(2)}) async-start(), calls=%async_computation.4 | async-start | bytes 4423680 | tf_op jit(solution)/shard_map/all_gather | solution.py:106
  52.9 26.8 %copy-start.1 = (bf16[240,768]{1,0:T(8,128)(2,1)S(1)}, bf16[240,768]{1,0:T(8,128)(2,1)}, u32[]{:S(2)}) copy-start(bf16[240,768]{1,0:T(8,128)(2,1)} %param.19) | copy-start | bytes 1105924
  52.9 94.1 %all-gather.12.cloned.1.call-start = ((), (), s32[]{:S(2)}) async-start(), calls=%async_computation.5 | async-start | bytes 1474560 | tf_op jit(solution)/shard_map/all_gather | solution.py:107
  53.4 126.2 %all-gather.14.cloned.1.call-start = ((), (), s32[]{:S(2)}) async-start(), calls=%async_computation.6 | async-start | bytes 5898240 | tf_op jit(solution)/shard_map/all_gather | solution.py:108
  54.0 154.6 %all-gather.16.cloned.1.call-start = ((), (), s32[]{:S(2)}) async-start(), calls=%async_computation.7 | async-start | bytes 5898240 | tf_op jit(solution)/shard_map/all_gather | solution.py:109
  54.6 179.4 %all-gather.20.cloned.1.call-start = ((), (), s32[]{:S(2)}) async-start(), calls=%async_computation.10 | async-start | bytes 1843200 | tf_op jit(solution)/shard_map/all_gather | solution.py:161
  57.9 26.2 %copy-start.38 = (f32[768]{0:T(1024)}, f32[768]{0:T(1024)S(1)}, u32[]{:S(2)}) copy-start(f32[768]{0:T(1024)S(1)} %get-tuple-element.25) | copy-start | bytes 9220
  80.8 35.6 %copy-start.49 = (f32[240]{0:T(256)}, f32[240]{0:T(256)S(1)}, u32[]{:S(2)}) copy-start(f32[240]{0:T(256)S(1)} %broadcast_multiply_fusion.8) | copy-start | bytes 2884
  82.1 34.4 %copy-start.54 = (f32[240]{0:T(256)}, f32[240]{0:T(256)S(1)}, u32[]{:S(2)}) copy-start(f32[240]{0:T(256)S(1)} %add_rsqrt_fusion.4) | copy-start | bytes 2884
  84.1 191.2 %reduce-scatter.9.cloned.1.call-start = ((), (), s32[]{:S(2)}) async-start(), calls=%async_computation.11 | async-start | bytes 1843200 | tf_op jit(solution)/shard_map/reduce_scatter | solution.py:169
  146.9 3.9 copy-start.17
  146.9 3.9 copy-start.60
  162.3 3.8 copy-start.19
  172.6 3.2 copy-start.18
  208.6 25.4 %copy-start.64 = (f32[768]{0:T(1024)S(1)}, f32[768]{0:T(1024)}, u32[]{:S(2)}) copy-start(f32[768]{0:T(1024)} %param.33) | copy-start | bytes 9220
  234.0 11.3 %copy-start.63 = (bf16[768,768]{1,0:T(8,128)(2,1)S(1)}, bf16[768,768]{1,0:T(8,128)(2,1)}, u32[]{:S(2)}) copy-start(bf16[768,768]{1,0:T(8,128)(2,1)} %param.34) | copy-start | bytes 3538948
  247.7 215.6 %all-gather.22.cloned.1.call-start = ((), (), s32[]{:S(2)}) async-start(), calls=%async_computation.12 | async-start | bytes 1843200 | tf_op jit(solution)/shard_map/all_gather | solution.py:215
  270.1 5.2 copy-start.2
  270.1 5.2 copy-start.5
  270.1 5.2 copy-start.39
  270.1 5.2 copy-start.56
  271.9 4.6 copy-start.45
  271.9 4.8 copy-start.51
  276.9 42.8 %copy-start.59 = (f32[15]{0:T(128)}, f32[15]{0:T(128)S(1)}, u32[]{:S(2)}) copy-start(f32[15]{0:T(128)S(1)} %add_rsqrt_fusion.6) | copy-start | bytes 184
  437.9 4.3 collective-permute-start
  439.2 3.0 collective-permute-start.1
  444.1 57.5 %copy-start.28 = (f32[15,768]{1,0:T(8,128)}, f32[15,768]{1,0:T(8,128)S(1)}, u32[]{:S(2)}) copy-start(f32[15,768]{1,0:T(8,128)S(1)} %subtract_multiply_fusion.1) | copy-start | bytes 138244
  445.0 55.1 %reduce-scatter.11.cloned.1.call-start = ((), (), s32[]{:S(2)}) async-start(), calls=%async_computation.13 | async-start | bytes 1843200 | tf_op jit(solution)/shard_map/reduce_scatter | solution.py:223
  470.1 30.0 %copy-start.44 = (f32[768]{0:T(1024)S(1)}, f32[768]{0:T(1024)}, u32[]{:S(2)}) copy-start(f32[768]{0:T(1024)} %copy-done.43) | copy-start | bytes 9220
  470.1 30.0 %copy-start.50 = (f32[240]{0:T(256)S(1)}, f32[240]{0:T(256)}, u32[]{:S(2)}) copy-start(f32[240]{0:T(256)} %copy-done.49) | copy-start | bytes 2884
  470.1 30.0 %copy-start.55 = (f32[240]{0:T(256)S(1)}, f32[240]{0:T(256)}, u32[]{:S(2)}) copy-start(f32[240]{0:T(256)} %copy-done.54) | copy-start | bytes 2884
  472.5 32.6 %copy-start.32 = (f32[60,3,16]{2,1,0:T(4,128)S(1)}, f32[60,3,16]{2,1,0:T(4,128)}, u32[]{:S(2)}) copy-start(f32[60,3,16]{2,1,0:T(4,128)} %copy-done.31) | copy-start | bytes 34564
  472.5 32.6 %copy-start.34 = (f32[60,3,16]{2,1,0:T(4,128)S(1)}, f32[60,3,16]{2,1,0:T(4,128)}, u32[]{:S(2)}) copy-start(f32[60,3,16]{2,1,0:T(4,128)} %copy-done.33) | copy-start | bytes 34564
  472.6 51.4 %all-gather.24.cloned.1.call-start = ((), (), s32[]{:S(2)}) async-start(), calls=%async_computation.14 | async-start | bytes 1843200 | tf_op jit(solution)/shard_map/all_gather | solution.py:232
  503.9 25.1 %copy-start.4 = (f32[60,3,16,16]{2,3,1,0:T(8,128)S(1)}, f32[60,3,16,16]{2,3,1,0:T(8,128)}, u32[]{:S(2)}) copy-start(f32[60,3,16,16]{2,3,1,0:T(8,128)} %copy-done.3) | copy-start | bytes 552964
  504.7 72.2 %reduce-scatter.13.cloned.1.call-start = ((), (), s32[]{:S(2)}) async-start(), calls=%async_computation.15 | async-start | bytes 1843200 | tf_op jit(solution)/shard_map/reduce_scatter | solution.py:269
  529.0 2.3 copy-start.8
  529.0 2.3 copy-start.22
  535.9 8.2 copy-start.15
  549.4 265.5 %all-reduce.7.cloned.1.call-start = ((), (), s32[]{:S(2)}) async-start(), calls=%async_computation.16 | async-start | bytes 14155776 | tf_op jit(solution)/shard_map/psum | solution.py:278
  549.6 4.8 copy-start.62
  549.6 4.8 copy-start.67
  554.4 2.9 copy-start.10
  554.4 2.9 copy-start.24
  554.5 4.2 copy-start.35
  554.5 4.2 copy-start.36
  554.5 4.2 copy-start.61
  561.0 15.9 %copy-start.42 = (f32[768]{0:T(1024)S(1)}, f32[768]{0:T(1024)}, u32[]{:S(2)}) copy-start(f32[768]{0:T(1024)} %copy-done.41) | copy-start | bytes 9220
  561.0 15.9 %copy-start.48 = (f32[240]{0:T(256)S(1)}, f32[240]{0:T(256)}, u32[]{:S(2)}) copy-start(f32[240]{0:T(256)} %copy-done.47) | copy-start | bytes 2884
  561.0 15.9 %copy-start.53 = (f32[240]{0:T(256)S(1)}, f32[240]{0:T(256)}, u32[]{:S(2)}) copy-start(f32[240]{0:T(256)} %copy-done.52) | copy-start | bytes 2884
  561.0 83.7 %copy-start.7 = (f32[240,768]{1,0:T(8,128)S(1)}, f32[240,768]{1,0:T(8,128)}, u32[]{:S(2)}) copy-start(f32[240,768]{1,0:T(8,128)} %copy-done.6) | copy-start | bytes 2211844
  814.9 3.0 copy-start.30
  814.9 3.8 copy-start.21
  817.8 2.2 copy-start.20
  (19 other events, 25.8 us)
Sparse Core Ops, SparseCore 0:
  13.2 21.7 all-gather.17
  52.2 27.3 reduce-scatter.6
  81.2 30.7 all-gather.9
  113.4 17.4 all-gather.11
  132.3 37.4 all-gather.13
  171.2 37.4 all-gather.15
  210.8 19.0 all-gather.19
  247.9 27.3 reduce-scatter.8
  445.1 18.2 all-gather.21
  472.7 27.3 reduce-scatter.10
  504.8 19.0 all-gather.23
  549.5 27.3 reduce-scatter.12
  581.9 232.9 all-reduce.6
where the time goes:
time: 839 us; the launch traced here: 829 us
  waiting for transfers between devices  347 us (41%)
  blocking collectives  222 us (26%)
  matrix products  125 us (15%)
  local copies, waits for them, and re-layouts  74.8 us (9%)
  other arithmetic  38.1 us (5%)
  between operations  18.9 us (2%)
    psum x1, waiting for transfers between devices, local(): lax.psum((grad_qkv, grad_qv_bias, grad_out, grad_fc1, grad_fc1_bias, grad...  168 us
    psum x2, blocking collectives, local(): summed, scalar = lax.psum((partial_value, own_term), ('dp', 'mp'))  78.7 us
    unnamed x1, blocking collectives  77.1 us
    dot_general x2, matrix products, image_tower(): result = middle + jnp.dot(active, w_fc2, preferred_element_type=jnp.float32)  45.9 us
    all_gather x1, blocking collectives, local(): arrived = lax.all_gather(captions16, ('dp', 'mp'), axis=0, tiled=True)  42.7 us
    all_gather x1, waiting for transfers between devices, local(): lax.all_gather(img_fc2, 'mp', axis=0, tiled=True)  29 us
    all_gather x1, waiting for transfers between devices, local(): lax.all_gather(img_qkv, 'mp', axis=2, tiled=True)  27.8 us
    reduce_scatter x1, waiting for transfers between devices, local(): lax.psum_scatter(jnp.einsum('gf,df->gd', grad_hidden16, txt_fc1, preferre...  27.5 us
  transfers between devices with their start and end apart: 15, of which 11 were waited for; matrix products, arithmetic and copies ran while one was open for 18% of the time, Pallas kernels for 0%

commit v1 on v0

--- a/solution.py
+++ b/solution.py
@@ -129,7 +129,21 @@
     unit1, inverse1 = layer_stats(inputs)
     normed1 = (unit1 * txt_gains[0] + txt_shifts[0]).astype(jnp.bfloat16)
     bias_rows = jnp.stack([txt_qv_bias[0], jnp.zeros_like(txt_qv_bias[0]), txt_qv_bias[1]])
-    piece = lax.all_gather(normed1, "mp", axis=0, tiled=True)
+    ways, here, lap = (lax.axis_size("mp"), lax.axis_index("mp"), normed1.shape[0])
+    dims = [n * ways if d == 0 else n for d, n in enumerate(normed1.shape)]
+    full = lax.dynamic_update_slice_in_dim(
+        jnp.zeros(dims, normed1.dtype), normed1, here * lap, axis=0
+    )
+    going_up = going_down = normed1
+    for far in range(1, ways // 2 + 1):
+        going_up = lax.ppermute(going_up, "mp", [(d, (d + 1) % ways) for d in range(ways)])
+        full = lax.dynamic_update_slice_in_dim(full, going_up, (here - far) % ways * lap, axis=0)
+        if 2 * far < ways:
+            going_down = lax.ppermute(going_down, "mp", [(d, (d - 1) % ways) for d in range(ways)])
+            full = lax.dynamic_update_slice_in_dim(
+                full, going_down, (here + far) % ways * lap, axis=0
+            )
+    piece = full
     made = jnp.einsum("rd,jdw->rjw", piece, txt_qkv, preferred_element_type=jnp.float32) + bias_rows
     joined = jnp.concatenate(
         [piece, made.astype(jnp.bfloat16).reshape(piece.shape[0], 3 * width)], 1

time: 839 us -> 844 us (level)
  waiting for transfers between devices: 347 us -> 337 us
    all_gather x1 -> x0, waiting for transfers between devices: 20.2 us -> none  [local(): piece = lax.all_gather(normed1, 'mp', axis=0, tiled=True)]
    dot_general x1, matrix products: 10.1 us -> 21.7 us  [local(): jnp.dot(piece, txt_fc1, preferred_element_type=jnp.float32) + txt_fc1_bias]
    ppermute x0 -> x3, waiting for transfers between devices: none -> 10.6 us  [the longest x2 10.6 us: local(): lax.ppermute(going_up, 'mp', [(d, (d + 1) % ways) for d in range(ways)])]
    reduce_scatter x1, waiting for transfers between devices: 20.6 us -> 29.2 us  [local(): lax.psum_scatter(jnp.dot(context, txt_out, preferred_element_type=jnp.flo...]
  transfers between devices with their start and end apart: 15 -> 17, of which waited for: 11 -> 11; matrix products, arithmetic and copies ran while one was open for 18% -> 20% of each run, Pallas kernels for 0% -> 0%
where the time goes in v1:
time: 844 us; the launch traced here: 836 us
  waiting for transfers between devices  337 us (40%)
  blocking collectives  222 us (26%)
  matrix products  129 us (15%)
  local copies, waits for them, and re-layouts  75.3 us (9%)
  other arithmetic  44.6 us (5%)
  between operations  19.8 us (2%)
  starting transfers between devices  8.93 us (1%)
    psum x1, waiting for transfers between devices, local(): lax.psum((grad_qkv, grad_qv_bias, grad_out, grad_fc1, grad_fc1_bias, grad...  168 us
    psum x2, blocking collectives, local(): summed, scalar = lax.psum((partial_value, own_term), ('dp', 'mp'))  78.5 us
    unnamed x1, blocking collectives  77.1 us
    dot_general x2, matrix products, image_tower(): result = middle + jnp.dot(active, w_fc2, preferred_element_type=jnp.float32)  46 us
    all_gather x1, blocking collectives, local(): arrived = lax.all_gather(captions16, ('dp', 'mp'), axis=0, tiled=True)  43 us
    reduce_scatter x1, waiting for transfers between devices, local(): lax.psum_scatter(jnp.dot(context, txt_out, preferred_element_type=jnp.flo...  29.2 us
    all_gather x1, waiting for transfers between devices, local(): lax.all_gather(img_fc2, 'mp', axis=0, tiled=True)  27.8 us
    reduce_scatter x1, waiting for transfers between devices, local(): lax.psum_scatter(jnp.einsum('gf,df->gd', grad_hidden16, txt_fc1, preferre...  27.5 us
  transfers between devices with their start and end apart: 17, of which 11 were waited for; matrix products, arithmetic and copies ran while one was open for 20% of the time, Pallas kernels for 0%

profile of v1, /device:TPU:0, one launch (start us, length us, event | category | flops | bytes accessed | tf_op | source)
XLA Modules:
  0.0 835.9 jit_solution(4249397023026670992)
XLA Ops:
  10.7 2.0 constant_dynamic-update-slice_fusion.3
  13.2 2.0 collective-permute-start.1
  15.5 6.4 collective-permute-done
  21.9 2.6 collective-permute-start.2
  24.6 4.2 collective-permute-done.2
  28.9 2.8 fusion.232
  32.9 1.9 copy.127
  34.8 3.0 reshape_reshape.3
  37.8 3.2 fusion.222
  44.5 1.7 convolution_convert_fusion.2
  48.3 29.2 %reduce-scatter.7.cloned.1.call-done = bf16[240,768]{1,0:T(8,128)(2,1)} async-done(((bf16[960,768]{1,0:T(8,128)(2,1)}), bf16[240,768]{1,0:T(8,128)(2,1)}) %reduce-scatter.7.cloned.1.call-update) | async-done | bytes 368656 | tf_op jit(solution)/shard_map/reduce_scatter | solution.py:165
  80.2 1.9 add_convert_fusion.2
  84.9 1.5 fusion.72
  89.6 20.3 %all-gather.9.cloned.1.call-done = bf16[3,768,768]{1,2,0:T(8,128)(2,1)} async-done(((bf16[3,768,192]{1,2,0:T(8,128)(2,1)}), bf16[3,768,768]{1,2,0:T(8,128)(2,1)}) %all-gather.9.cloned.1.call-update) | async-done | bytes 3538960 | tf_op jit(solution)/shard_map/all_gather | solution.py:106
  109.9 4.5 convert_bitcast_fusion
  115.8 1.5 copy-done.67
  117.3 1.9 convert_bitcast_fusion.2
  120.4 2.3 reshape.235
  122.7 3.1 squeeze.29
  125.8 2.5 reshape.237
  128.3 3.3 reshape.236
  131.6 2.4 fusion.65
  134.0 5.2 fusion.228
  141.3 2.0 reshape.222
  143.3 4.1 squeeze.31
  147.4 2.8 squeeze.30
  150.2 3.8 fusion.45
  154.0 6.8 fusion.230
  162.1 1.8 copy.118
  163.9 4.2 reshape.220
  168.1 2.5 fusion.229
  174.7 21.7 %multiply_convert_fusion = (bf16[960,768]{1,0:T(8,128)(2,1)S(1)}, f32[960,768]{1,0:T(8,128)}, f32[960,768]{1,0:T(8,128)}) fusion(f32[768]{0:T(1024)S(1)} %copy-done.71, bf16[960,768]{1,0:T(8,128)(2,1)} %all-gather.17.cloned.1.call-done, bf16[768,768]{1,0:T(8,128)(2,1)S(1)} %copy-done), kind=kOutput, calls=%fused_computation.54 | convolution fusion | flops 1181122560 | bytes 10030080 | tf_op jit(solution)/shard_map/dot_general | solution.py:176
  197.5 2.4 convolution_convert_fusion.1
  200.0 27.8 %all-gather.15.cloned.1.call-done = bf16[3072,768]{1,0:T(8,128)(2,1)} async-done(((bf16[768,768]{1,0:T(8,128)(2,1)}), bf16[3072,768]{1,0:T(8,128)(2,1)}) %all-gather.15.cloned.1.call-update) | async-done | bytes 4718608 | tf_op jit(solution)/shard_map/all_gather | solution.py:109
  227.8 25.5 %fusion.58 = f32[600,768]{1,0:T(8,128)} fusion(f32[600,768]{1,0:T(8,128)S(1)} %copy-done.25, bf16[3072,768]{1,0:T(8,128)(2,1)} %all-gather.15.cloned.1.call-done, bf16[768,3072]{1,0:T(8,128)(2,1)} %all-gather.13.cloned.1.call-done, f32[768]{0:T(1024)S(1)} %get-tuple-element.22, f32[600]{0:T(1024)S(1)} %add_rsqrt_fusion, f32[600]{0:T(1024)S(1)} %broadcast_multiply_fusion), kind=kOutput, calls=%fused_computation.102 | convolution fusion | flops 5784422400 | bytes 13131456 | tf_op jit(solution)/shard_map/dot_general | solution.py:77
  253.3 20.6 %fusion.62 = f32[435,768]{1,0:T(8,128)} fusion(f32[435,768]{1,0:T(8,128)} %copy-done.30, bf16[3072,768]{1,0:T(8,128)(2,1)} %all-gather.15.cloned.1.call-done, bf16[768,3072]{1,0:T(8,128)(2,1)} %all-gather.13.cloned.1.call-done, f32[768]{0:T(1024)S(1)} %get-tuple-element.22, f32[435]{0:T(512)S(1)} %add_rsqrt_fusion.2, f32[435]{0:T(512)S(1)} %broadcast_multiply_fusion.2), kind=kOutput, calls=%fused_computation.115 | convolution fusion | flops 4193706240 | bytes 12116376 | tf_op jit(solution)/shard_map/dot_general | solution.py:77
  273.9 1.5 reshape.223
  275.5 2.8 reshape.221
  278.3 1.8 reduce_sum.383
  282.8 43.0 %all-gather = bf16[32,15,768]{2,1,0:T(8,128)(2,1)S(1)} all-gather(bf16[1,15,768]{2,1,0:T(8,128)(2,1)S(1)} %fusion.139), channel_id=1, replica_groups=mesh['dp'=8,'mp'=4] {'dp','mp'}, dimensions={0}, use_global_device_ids=true | all-gather | bytes 760320 | tf_op jit(solution)/shard_map/all_gather | solution.py:199
  326.0 1.6 fusion.137
  327.7 36.8 %psum.64 = f32[480]{0:T(512)S(1)} all-reduce(f32[480]{0:T(512)S(1)} %get-tuple-element.19), channel_id=1, replica_groups=mesh['dp'=8,'mp'=4] {'dp','mp'}, use_global_device_ids=true, to_apply=%region_32.33 | all-reduce | flops 480 | bytes 3840 | tf_op jit(solution)/shard_map/psum | solution.py:207
  366.9 77.1 %fusion = f32[16,768]{1,0:T(8,128)S(1)} fusion(f32[480,768]{1,0:T(8,128)S(1)} %convolution_multiply_fusion), kind=kCustom, calls=%all-reduce-scatter | all-reduce-scatter fusion | flops 393217 | bytes 1523712
  451.1 18.3 %all-gather.19.cloned.1.call-done = bf16[960,768]{1,0:T(8,128)(2,1)} async-done(((bf16[240,768]{1,0:T(8,128)(2,1)}), bf16[960,768]{1,0:T(8,128)(2,1)}) %all-gather.19.cloned.1.call-update) | async-done | bytes 1474576 | tf_op jit(solution)/shard_map/all_gather | solution.py:229
  469.5 5.6 convert_reduce_fusion
  476.2 2.5 convolution_convert_fusion
  478.7 27.5 %reduce-scatter.11.cloned.1.call-done = bf16[240,768]{1,0:T(8,128)(2,1)} async-done(((bf16[960,768]{1,0:T(8,128)(2,1)}), bf16[240,768]{1,0:T(8,128)(2,1)}) %reduce-scatter.11.cloned.1.call-update) | async-done | bytes 368656 | tf_op jit(solution)/shard_map/reduce_scatter | solution.py:237
  506.3 1.5 fusion.114
  511.9 18.2 %all-gather.21.cloned.1.call-done = bf16[960,768]{1,0:T(8,128)(2,1)} async-done(((bf16[240,768]{1,0:T(8,128)(2,1)}), bf16[960,768]{1,0:T(8,128)(2,1)}) %all-gather.21.cloned.1.call-update) | async-done | bytes 1474576 | tf_op jit(solution)/shard_map/all_gather | solution.py:246
  530.1 2.8 convolution_convert_fusion.5
  535.2 2.3 multiply_reduce_fusion.3
  543.3 2.0 copy.144
  545.3 1.6 copy.139
  548.3 2.0 copy.143
  551.6 3.9 bitcast_convert_fusion
  555.9 4.8 fusion.235
  560.7 2.8 fusion.234
  564.9 2.3 convolution_bitcast_fusion
  569.6 13.4 %reduce-scatter.13.cloned.1.call-done = bf16[240,768]{1,0:T(8,128)(2,1)} async-done(((bf16[960,768]{1,0:T(8,128)(2,1)}), bf16[240,768]{1,0:T(8,128)(2,1)}) %reduce-scatter.13.cloned.1.call-update) | async-done | bytes 368656 | tf_op jit(solution)/shard_map/reduce_scatter | solution.py:283
  584.5 23.1 %all-reduce.3 = (f32[2,192]{1,0:T(2,128)}, f32[768]{0:T(1024)}) all-reduce(f32[2,192]{1,0:T(2,128)S(1)} %pad_maximum_fusion.7, f32[768]{0:T(1024)S(1)} %get-tuple-element.38), channel_id=1, replica_groups=mesh['dp'=8,'mp'=4] {'dp'}, use_global_device_ids=true, to_apply=%region_46.47 | all-reduce | flops 1152 | bytes 9216 | tf_op jit(solution)/shard_map/psum | solution.py:292
  607.7 41.7 %all-reduce.2 = (f32[]{:T(128)}, f32[6,768]{1,0:T(8,128)S(1)}) all-reduce(f32[]{:T(128)S(6)} %sub.165, f32[6,768]{1,0:T(8,128)S(1)} %stack.59), channel_id=1, replica_groups=mesh['dp'=8,'mp'=4] {'dp','mp'}, use_global_device_ids=true, to_apply=%region_30.31 | all-reduce | flops 4609 | bytes 36872 | tf_op jit(solution)/shard_map/psum | solution.py:207
  650.6 2.2 fusion.107
  652.8 168.0 %all-reduce.7.cloned.1.call-done = (f32[3,768,192]{1,2,0:T(8,128)}, f32[192,768]{1,0:T(8,128)}, f32[768,768]{1,0:T(8,128)}, f32[768,768]{1,0:T(8,128)}) async-done(((f32[3,768,192]{1,2,0:T(8,128)}, f32[192,768]{1,0:T(8,128)}, f32[768,768]{1,0:T(8,128)}, f32[768,768]{1,0:T(8,128)}), (f32[3,768,192]{1,2,0:T(8,128)}, f32[192,768]{1,0:T(8,128)}, f32[768,768]{1,0:T(8,128)}, ...) | async-done | bytes 7077904 | tf_op jit(solution)/shard_map/psum | solution.py:292
  820.9 2.9 copy.209
  (291 shorter events, 66.9 us)
Async XLA Ops:
  7.2 167.5 %copy-start = (bf16[768,768]{1,0:T(8,128)(2,1)S(1)}, bf16[768,768]{1,0:T(8,128)(2,1)}, u32[]{:S(2)}) copy-start(bf16[768,768]{1,0:T(8,128)(2,1)} %param.32) | copy-start | bytes 3538948
  7.2 8.0 copy-start.52
  7.2 8.0 copy-start.66
  7.2 70.4 %reduce-scatter.7.cloned.1.call-start = ((), (), s32[]{:S(2)}) async-start(), calls=%async_computation.8 | async-start | bytes 1843200 | tf_op jit(solution)/shard_map/reduce_scatter | solution.py:165
  8.5 4.2 copy-start.55
  10.5 69.6 %copy-start.49 = (f32[768]{0:T(1024)}, f32[768]{0:T(1024)S(1)}, u32[]{:S(2)}) copy-start(f32[768]{0:T(1024)S(1)} %get-tuple-element.84) | copy-start | bytes 9220
  12.7 9.2 %collective-permute-start = (bf16[240,768]{1,0:T(8,128)(2,1)}, bf16[240,768]{1,0:T(8,128)(2,1)S(1)}, u32[]{:S(2)}, u32[]{:S(2)}) collective-permute-start(bf16[240,768]{1,0:T(8,128)(2,1)} %get-tuple-element.47), channel_id=1, source_target_pairs={{0,1},{1,2},{2,3},{3,0},{4,5},{5,6},{6,7},{7,4},{8,9},{9,10},{10,1... | collective-permute-start | bytes 1105928 | tf_op jit(solution)/shard_map/ppermute | solution.py:139
  13.2 11.4 %collective-permute-start.1 = (bf16[240,768]{1,0:T(8,128)(2,1)}, bf16[240,768]{1,0:T(8,128)(2,1)S(1)}, u32[]{:S(2)}, u32[]{:S(2)}) collective-permute-start(bf16[240,768]{1,0:T(8,128)(2,1)} %get-tuple-element.47), channel_id=1, source_target_pairs={{0,3},{1,0},{2,1},{3,2},{4,7},{5,4},{6,5},{7,6},{8,11},{9,8},{10,9... | collective-permute-start | bytes 1105928 | tf_op jit(solution)/shard_map/ppermute | solution.py:142
  21.9 6.9 collective-permute-start.2
  43.8 3.9 copy-start.63
  43.8 33.8 %copy-start.1 = (bf16[240,768]{1,0:T(8,128)(2,1)S(1)}, bf16[240,768]{1,0:T(8,128)(2,1)}, u32[]{:S(2)}) copy-start(bf16[240,768]{1,0:T(8,128)(2,1)} %param.19) | copy-start | bytes 1105924
  44.5 35.6 %copy-start.9 = (bf16[960,192]{1,0:T(8,128)(2,1)}, bf16[960,192]{1,0:T(8,128)(2,1)S(1)}, u32[]{:S(2)}) copy-start(bf16[960,192]{1,0:T(8,128)(2,1)S(1)} %reshape.224) | copy-start | bytes 1105924
  46.2 63.7 %all-gather.9.cloned.1.call-start = ((), (), s32[]{:S(2)}) async-start(), calls=%async_computation.4 | async-start | bytes 4423680 | tf_op jit(solution)/shard_map/all_gather | solution.py:106
  46.9 121.2 %all-gather.11.cloned.1.call-start = ((), (), s32[]{:S(2)}) async-start(), calls=%async_computation.5 | async-start | bytes 1474560 | tf_op jit(solution)/shard_map/all_gather | solution.py:107
  47.7 127.0 %all-gather.17.cloned.1.call-start = ((), (), s32[]{:S(2)}) async-start(), calls=%async_computation.9 | async-start | bytes 1843200 | tf_op jit(solution)/shard_map/all_gather | solution.py:175
  48.3 36.5 %copy-start.44 = (f32[768]{0:T(1024)}, f32[768]{0:T(1024)S(1)}, u32[]{:S(2)}) copy-start(f32[768]{0:T(1024)S(1)} %get-tuple-element.25) | copy-start | bytes 9220
  78.8 7.6 copy-start.53
  78.8 7.6 copy-start.11
  80.1 6.4 copy-start.58
  82.1 4.9 copy-start.64
  82.1 117.9 %all-gather.13.cloned.1.call-start = ((), (), s32[]{:S(2)}) async-start(), calls=%async_computation.6 | async-start | bytes 5898240 | tf_op jit(solution)/shard_map/all_gather | solution.py:108
  82.7 145.1 %all-gather.15.cloned.1.call-start = ((), (), s32[]{:S(2)}) async-start(), calls=%async_computation.7 | async-start | bytes 5898240 | tf_op jit(solution)/shard_map/all_gather | solution.py:109
  83.3 197.8 %reduce-scatter.9.cloned.1.call-start = ((), (), s32[]{:S(2)}) async-start(), calls=%async_computation.10 | async-start | bytes 1843200 | tf_op jit(solution)/shard_map/reduce_scatter | solution.py:183
  87.7 22.2 %copy-start.46 = (f32[15,16]{0,1:T(8,128)}, f32[15,16]{0,1:T(8,128)S(1)}, u32[]{:S(2)}) copy-start(f32[15,16]{0,1:T(8,128)S(1)} %get-tuple-element.43) | copy-start | bytes 2884
  134.0 5.2 copy-start.26
  143.3 4.2 copy-start.13
  154.0 6.8 copy-start.20
  162.1 6.0 copy-start.19
  168.1 3.9 copy-start.12
  168.1 3.9 copy-start.33
  168.1 3.9 copy-start.70
  174.7 22.8 %copy-start.69 = (bf16[768,768]{1,0:T(8,128)(2,1)S(1)}, bf16[768,768]{1,0:T(8,128)(2,1)}, u32[]{:S(2)}) copy-start(bf16[768,768]{1,0:T(8,128)(2,1)} %param.34) | copy-start | bytes 3538948
  197.5 30.3 %copy-start.25 = (f32[600,768]{1,0:T(8,128)S(1)}, f32[600,768]{1,0:T(8,128)}, u32[]{:S(2)}) copy-start(f32[600,768]{1,0:T(8,128)} %copy-done.24) | copy-start | bytes 5529604
  200.0 269.5 %all-gather.19.cloned.1.call-start = ((), (), s32[]{:S(2)}) async-start(), calls=%async_computation.11 | async-start | bytes 1843200 | tf_op jit(solution)/shard_map/all_gather | solution.py:229
  275.5 5.6 copy-start.2
  275.5 5.6 copy-start.5
  275.5 5.6 copy-start.45
  275.5 5.6 copy-start.60
  278.3 4.0 copy-start.51
  278.3 4.2 copy-start.57
  282.7 43.1 %copy-start.65 = (f32[15]{0:T(128)}, f32[15]{0:T(128)S(1)}, u32[]{:S(2)}) copy-start(f32[15]{0:T(128)S(1)} %add_rsqrt_fusion.6) | copy-start | bytes 184
  444.0 4.3 collective-permute-start.3
  445.3 3.0 collective-permute-start.4
  450.2 57.5 %copy-start.34 = (f32[15,768]{1,0:T(8,128)}, f32[15,768]{1,0:T(8,128)S(1)}, u32[]{:S(2)}) copy-start(f32[15,768]{1,0:T(8,128)S(1)} %subtract_multiply_fusion.1) | copy-start | bytes 138244
  451.1 55.2 %reduce-scatter.11.cloned.1.call-start = ((), (), s32[]{:S(2)}) async-start(), calls=%async_computation.12 | async-start | bytes 1843200 | tf_op jit(solution)/shard_map/reduce_scatter | solution.py:237
  476.2 30.1 %copy-start.50 = (f32[768]{0:T(1024)S(1)}, f32[768]{0:T(1024)}, u32[]{:S(2)}) copy-start(f32[768]{0:T(1024)} %copy-done.49) | copy-start | bytes 9220
  476.2 30.1 %copy-start.54 = (f32[240]{0:T(256)S(1)}, f32[240]{0:T(256)}, u32[]{:S(2)}) copy-start(f32[240]{0:T(256)} %copy-done.53) | copy-start | bytes 2884
  476.2 30.1 %copy-start.59 = (f32[240]{0:T(256)S(1)}, f32[240]{0:T(256)}, u32[]{:S(2)}) copy-start(f32[240]{0:T(256)} %copy-done.58) | copy-start | bytes 2884
  478.7 32.5 %copy-start.38 = (f32[60,3,16]{2,1,0:T(4,128)S(1)}, f32[60,3,16]{2,1,0:T(4,128)}, u32[]{:S(2)}) copy-start(f32[60,3,16]{2,1,0:T(4,128)} %copy-done.37) | copy-start | bytes 34564
  478.7 32.5 %copy-start.40 = (f32[60,3,16]{2,1,0:T(4,128)S(1)}, f32[60,3,16]{2,1,0:T(4,128)}, u32[]{:S(2)}) copy-start(f32[60,3,16]{2,1,0:T(4,128)} %copy-done.39) | copy-start | bytes 34564
  478.7 51.4 %all-gather.21.cloned.1.call-start = ((), (), s32[]{:S(2)}) async-start(), calls=%async_computation.13 | async-start | bytes 1843200 | tf_op jit(solution)/shard_map/all_gather | solution.py:246
  510.1 25.1 %copy-start.4 = (f32[60,3,16,16]{2,3,1,0:T(8,128)S(1)}, f32[60,3,16,16]{2,3,1,0:T(8,128)}, u32[]{:S(2)}) copy-start(f32[60,3,16,16]{2,3,1,0:T(8,128)} %copy-done.3) | copy-start | bytes 552964
  510.9 72.2 %reduce-scatter.13.cloned.1.call-start = ((), (), s32[]{:S(2)}) async-start(), calls=%async_computation.14 | async-start | bytes 1843200 | tf_op jit(solution)/shard_map/reduce_scatter | solution.py:283
  542.0 8.3 copy-start.17
  555.5 265.4 %all-reduce.7.cloned.1.call-start = ((), (), s32[]{:S(2)}) async-start(), calls=%async_computation.15 | async-start | bytes 14155776 | tf_op jit(solution)/shard_map/psum | solution.py:292
  555.8 4.8 copy-start.68
  555.9 4.8 copy-start.74
  560.7 4.2 copy-start.29
  560.7 4.2 copy-start.41
  560.7 4.2 copy-start.42
  567.2 15.8 %copy-start.48 = (f32[768]{0:T(1024)S(1)}, f32[768]{0:T(1024)}, u32[]{:S(2)}) copy-start(f32[768]{0:T(1024)} %copy-done.47) | copy-start | bytes 9220
  567.2 15.8 %copy-start.56 = (f32[240]{0:T(256)S(1)}, f32[240]{0:T(256)}, u32[]{:S(2)}) copy-start(f32[240]{0:T(256)} %copy-done.55) | copy-start | bytes 2884
  567.2 15.8 %copy-start.62 = (f32[240]{0:T(256)S(1)}, f32[240]{0:T(256)}, u32[]{:S(2)}) copy-start(f32[240]{0:T(256)} %copy-done.61) | copy-start | bytes 2884
  567.2 83.4 %copy-start.7 = (f32[240,768]{1,0:T(8,128)S(1)}, f32[240,768]{1,0:T(8,128)}, u32[]{:S(2)}) copy-start(f32[240,768]{1,0:T(8,128)} %copy-done.6) | copy-start | bytes 2211844
  (28 other events, 55.4 us)
Sparse Core Ops, SparseCore 0:
  46.3 31.2 reduce-scatter.6
  79.1 30.7 all-gather.8
  111.5 17.4 all-gather.10
  130.9 19.0 all-gather.16
  151.5 37.4 all-gather.12
  190.4 37.4 all-gather.14
  231.0 27.4 reduce-scatter.8
  451.2 18.2 all-gather.18
  478.8 27.3 reduce-scatter.10
  511.0 19.0 all-gather.20
  555.6 27.3 reduce-scatter.12
  587.9 232.9 all-reduce.6
